TPU v7x, 32 devices: a whole 2x2x4 slice. The times are simulated.
32 devices in a mesh: rows: 8 (over z, y), vecs: 4 (over x, core).
Axes of the slice: x: 2, y: 2, z: 4, core: 2. Of those that a mesh axis runs over, the one named last changes fastest.
Arguments:
- basis: bfloat16 [100, 524288], P('vecs', 'rows'), may hold values from -6 to 6
- coefficients: bfloat16 [100, 40], replicated, may hold values from -0.625 to 0.625
- eigen_values: float32 [40], P('vecs'), may hold values from -3 to 1
- stiffness: float32 [524288], P('rows'), may hold values from 6.5 to 10
- damping: float32 [524288], P('rows'), may hold values from 0.2 to 2
- mass: float32 [524288], P('rows'), may hold values from 0.5 to 2
- link_count: int32 [8], P('rows'), may hold values from 1024 to 4096, as said below
- lower_cells: int32 [8, 4096], P('rows'), may hold values from 0 to 4095
- upper_cells: int32 [8, 4096], P('rows'), may hold values from 0 to 4095
Outputs:
- eigvecs: bfloat16 [40, 524288], P('vecs', 'rows')
- residuals: bfloat16 [40, 524288], P('vecs', 'rows')
- relative_norms: float32 [40], P('vecs')
Inputs may be any that keep to these rules, and one draw needn't show every extreme that they name: Interface s joins subdomain s to subdomain (s + 1) mod 8; only its first link_count[s] slots are used, the others are to be ignored. Some interface uses all 4096 slots in every draw. `lower_cells`: slots beyond link_count[s] hold values that are not used. `upper_cells`: slots beyond link_count[s] hold values that are not used.
All inputs are finite; a program needn't handle non-finite values.
Results may differ from a plain program's by a relative error of at most 0.0037.
The roundings to bfloat16 on the way count: a program that leaves them out, or rounds other values in their place, can miss the bound.
Values may be sent and summed in bfloat16 or wider, within the bound.
A program may use at most 320 MiB of HBM per device.

v0:
```python
import jax
import jax.numpy as jnp
from jax import lax
from jax.sharding import PartitionSpec as P

WID = 64


def from_behind(value, axis, steps):
    count = lax.axis_size(axis)
    pairs = [(source, (source + steps) % count) for source in range(count)]
    return lax.ppermute(value, axis, pairs)


def neighbours(values, width_cells):
    depth_pad = jnp.pad(values, ((0, 0), (1, 1), (0, 0)))
    total = depth_pad[:, 2:] + depth_pad[:, :-2]
    across = jnp.pad(values, ((0, 0), (0, 0), (width_cells, width_cells)))
    total = total + across[:, :, 2 * width_cells :] + across[:, :, : -2 * width_cells]
    column = jnp.arange(values.shape[2]) % width_cells
    shifted = jnp.pad(values, ((0, 0), (0, 0), (1, 1)))
    total = total + jnp.where(column < width_cells - 1, shifted[:, :, 2:], 0.0)
    total = total + jnp.where(column > 0, shifted[:, :, :-2], 0.0)
    return total


def on_device(
    basis,
    coefficients,
    eigen_values,
    stiffness,
    damping,
    mass,
    link_count,
    lower_cells,
    upper_cells,
):
    vector_part = eigen_values.shape[0]
    rows_local = basis.shape[1]
    plane_cells = WID * WID
    plane_count = rows_local // plane_cells
    quarter = lax.all_to_all(basis, "vecs", split_axis=1, concat_axis=0, tiled=True)
    quarter_vecs = jnp.dot(coefficients.T, quarter, preferred_element_type=jnp.float32).astype(
        jnp.bfloat16
    )
    eigvecs = lax.all_to_all(quarter_vecs, "vecs", split_axis=0, concat_axis=1, tiled=True)
    vectors = eigvecs.astype(jnp.float32)
    vector_sq = lax.psum(jnp.sum(vectors * vectors, axis=1), "rows")
    down_lower, down_upper, down_count = from_behind(
        (lower_cells, upper_cells, link_count), "rows", 1
    )
    slot_index = jnp.arange(lower_cells.shape[1], dtype=jnp.int32)
    own_used = slot_index < link_count[0]
    down_used = slot_index < down_count[0]
    planes = eigvecs.reshape(vector_part, plane_count, plane_cells)
    last_plane = planes[:, plane_count - 1, :]
    first_plane = planes[:, 0, :]
    zero_value = jnp.zeros((), jnp.bfloat16)
    send_up = jnp.where(own_used[None, :], last_plane[:, lower_cells[0]], zero_value)
    send_down = jnp.where(down_used[None, :], first_plane[:, down_upper[0]], zero_value)
    from_below = from_behind(send_up, "rows", 1)
    from_above = from_behind(send_down, "rows", -1)
    link_first = (
        jnp.zeros((vector_part, plane_cells), jnp.float32)
        .at[:, down_upper[0]]
        .add(from_below.astype(jnp.float32))
    )
    link_last = (
        jnp.zeros((vector_part, plane_cells), jnp.float32)
        .at[:, lower_cells[0]]
        .add(from_above.astype(jnp.float32))
    )
    link_sum = jnp.zeros((vector_part, plane_count, plane_cells), jnp.float32)
    link_sum = link_sum.at[:, 0, :].add(link_first).at[:, plane_count - 1, :].add(link_last)
    neighbour_sum = neighbours(vectors.reshape(vector_part, plane_count, plane_cells), WID)
    total_coupled = (neighbour_sum + link_sum).reshape(vector_part, rows_local)
    eigen_col = eigen_values[:, None]
    diagonal = (
        eigen_col * eigen_col * mass[None, :] + eigen_col * damping[None, :] + stiffness[None, :]
    )
    coupling = eigen_col * eigen_col * 0.1 + eigen_col * 0.3 + 1.0
    residual_full = diagonal * vectors - coupling * total_coupled
    local_residual = jnp.sum(residual_full * residual_full, axis=1)
    residual_sq = lax.psum(local_residual, "rows")
    relative_norms = jnp.sqrt(residual_sq) / jnp.sqrt(vector_sq + 1.0)
    return (eigvecs, residual_full.astype(jnp.bfloat16), relative_norms)


def solution(mesh):
    placed = (
        P("vecs", "rows"),
        P(),
        P("vecs"),
        P("rows"),
        P("rows"),
        P("rows"),
        P("rows"),
        P("rows", None),
        P("rows", None),
    )
    return jax.shard_map(
        on_device,
        mesh=mesh,
        in_specs=placed,
        out_specs=(P("vecs", "rows"), P("vecs", "rows"), P("vecs")),
        check_vma=False,
    )
```

profile of v0, /device:TPU:0, one launch (start us, length us, event | category | flops | bytes accessed | tf_op | source)
XLA Modules:
  0.0 400.1 jit_solution(4268759849004805670)
XLA Ops:
  0.6 0.0 copy-start
  0.6 6.3 %all_to_all.30 = bf16[25,4,16384]{2,1,0:T(4,128)(2,1)S(1)} reshape(bf16[25,65536]{1,0:T(8,128)(2,1)} %param.13) | data formatting | bytes 6553600 | tf_op jit(solution)/shard_map/all_to_all | solution.py:42
  7.0 3.8 copy.25
  10.8 0.0 copy-start.15
  10.8 0.0 copy-start.14
  10.8 5.0 %all-to-all-start = ((bf16[25,4,16384]{2,0,1:T(8,128)(2,1)}), bf16[25,4,16384]{2,0,1:T(8,128)(2,1)}, u32[]{:S(2)}, u32[]{:S(2)}) async-start(bf16[25,4,16384]{2,0,1:T(8,128)(2,1)} %copy.25), calls=%async_computation | async-start | bytes 8388608 | tf_op jit(solution)/shard_map/all_to_all | solution.py:42
  15.8 0.0 copy-done.19
  15.8 3.0 collective-permute-start
  18.9 1.5 collective-permute-start.2
  21.1 0.0 copy-done.2
  21.1 0.8 add.124
  21.9 0.0 copy-done.4
  21.9 0.9 mul.101
  22.8 0.0 copy-done.6
  22.8 0.8 mul.97
  23.6 0.6 fusion.16
  24.2 0.0 copy-done.15
  24.2 0.5 add_add_fusion
  24.7 0.0 copy-done.14
  24.8 0.0 copy-start.10
  24.8 0.6 copy-done.10
  25.4 0.0 collective-permute-done.2
  25.4 1.2 iota_compare_fusion
  26.6 38.1 %all-to-all-done = bf16[25,4,16384]{2,0,1:T(8,128)(2,1)} async-done(((bf16[25,4,16384]{2,0,1:T(8,128)(2,1)}), bf16[25,4,16384]{2,0,1:T(8,128)(2,1)}, u32[]{:S(2)}, u32[]{:S(2)}) %all-to-all-start) | async-done | bytes 3276832 | tf_op jit(solution)/shard_map/all_to_all | solution.py:42
  64.7 3.3 all_to_all.33
  68.1 1.9 convolution_convert_fusion
  70.0 3.1 all_to_all.34
  73.1 3.6 all-to-all-start.1
  76.7 0.0 collective-permute-done
  76.8 0.0 copy-start.11
  76.8 25.6 %all-to-all-done.1 = bf16[4,10,16384]{2,1,0:T(8,128)(2,1)S(1)} async-done(((bf16[4,10,16384]{2,1,0:T(8,128)(2,1)}), bf16[4,10,16384]{2,1,0:T(8,128)(2,1)S(1)}, u32[]{:S(2)}, u32[]{:S(2)}) %all-to-all-start.1) | async-done | bytes 1310752 | tf_op jit(solution)/shard_map/all_to_all | solution.py:46
  102.3 11.0 %copy.27 = bf16[10,4,16384]{0,2,1:T(8,128)(2,1)} copy(bf16[10,4,16384]{2,0,1:T(8,128)(2,1)S(1)} %bitcast.40) | data formatting | bytes 2621440 | tf_op jit(solution)/shard_map/all_to_all | solution.py:46
  113.3 2.6 slice_bitcast_fusion
  116.0 15.0 %gather_fusion = bf16[4096,10]{1,0:T(8,128)(2,1)} fusion(bf16[10,4096]{0,1:T(8,128)(2,1)S(1)} %get-tuple-element.32, s32[4096]{0:T(1024)S(1)} %broadcast_clamp_fusion.1), kind=kCustom, calls=%fused_computation | custom fusion | bytes 180224 | tf_op jit(solution)/shard_map/gather | solution.py:59
  131.0 3.4 select_bitcast_fusion.1
  134.4 0.4 copy.28
  134.8 2.5 collective-permute-start.1
  137.3 12.4 %gather_fusion.1 = bf16[4096,10]{1,0:T(8,128)(2,1)S(1)} fusion(bf16[10,4096]{0,1:T(8,128)(2,1)} %get-tuple-element.31, s32[4096]{0:T(1024)S(1)} %broadcast_clamp_fusion), kind=kCustom, calls=%fused_computation.1 | custom fusion | bytes 180224 | tf_op jit(solution)/shard_map/gather | solution.py:60
  149.8 2.9 select_bitcast_fusion
  152.6 18.2 %convert_element_type.30 = f32[10,16,4096]{0,2,1:T(8,128)} convert(bf16[10,16,4096]{0,2,1:T(8,128)(2,1)} %bitcast.39) | non-fusion elementwise | flops 655360 | bytes 3932160 | tf_op jit(solution)/shard_map/convert_element_type | solution.py:47
  170.8 1.0 copy.26
  171.8 2.3 copy.30
  174.1 3.1 collective-permute-start.3
  177.2 0.8 pad.22
  177.9 2.5 copy.34
  180.4 0.0 collective-permute-done.1
  180.4 0.9 convert_bitcast_fusion.1
  181.3 2.0 copy.29
  183.3 24.1 %scatter_custom_fusion = f32[10,4096]{0,1:T(8,128)} fusion(s32[4096]{0:T(1024)} %bitcast.49, f32[4096,10]{1,0:T(8,128)} %copy.29, f32[]{:T(128)} %constant.81.clone.1), kind=kCustom, calls=%fused_computation.27 | custom fusion | flops 40960 | bytes 164352 | tf_op jit(solution)/shard_map/scatter-add | solution.py:66
  207.4 12.1 %scatter-add.25 = f32[10,16,4096]{0,2,1:T(8,128)} pad(f32[10,1,4096]{0,2,1:T(8,128)} %bitcast.44, f32[]{:T(128)} %constant.81.clone.1), padding=0_0x0_15x0_0 | pad | bytes 2785284 | tf_op jit(solution)/shard_map/scatter-add | solution.py:74
  219.5 0.0 collective-permute-done.3
  219.5 0.9 convert_bitcast_fusion
  220.4 0.0 copy-start.12
  220.4 2.0 copy.31
  222.4 24.1 %scatter_custom_fusion.1 = f32[10,4096]{0,1:T(8,128)} fusion(s32[4096]{0:T(1024)} %bitcast.47, f32[4096,10]{1,0:T(8,128)} %copy.31, f32[]{:T(128)} %constant.81.clone.1), kind=kCustom, calls=%fused_computation.25 | custom fusion | flops 40960 | bytes 164352 | tf_op jit(solution)/shard_map/scatter-add | solution.py:71
  246.5 3.0 bitcast_dynamic-update-slice_fusion
  249.5 82.5 %fusion.5 = f32[10,16,4096]{0,2,1:T(8,128)} fusion(f32[10,16,4096]{0,2,1:T(8,128)} %bitcast_dynamic-update-slice_fusion, f32[10,16,4096]{0,2,1:T(8,128)} %convert_element_type.30, pred[4096]{0:T(1024)(128)(4,1)S(1)} %get-tuple-element.35, pred[4096]{0:T(1024)(128)(4,1)S(1)} %copy-done.12), kind=kLoop, calls=%fused_computation.11 | loop fusion | flops 5242880 | bytes 7872512 | tf_op jit(solution)/shard_map/add | solution.py:76
  332.1 19.5 %copy.33 = f32[10,4,16384]{2,0,1:T(8,128)} copy(f32[10,4,16384]{0,2,1:T(8,128)} %bitcast.36) | data formatting | bytes 5242880 | tf_op jit(solution)/shard_map/reshape | solution.py:76
  351.6 19.5 %copy.32 = f32[10,65536]{1,0:T(8,128)} copy(f32[10,65536]{0,1:T(8,128)} %bitcast.37) | data formatting | bytes 5242880 | tf_op jit(solution)/shard_map/reshape | solution.py:76
  371.1 3.8 fusion.8
  374.9 19.1 %all-reduce.4 = (f32[10]{0:T(128)S(1)}, f32[10]{0:T(128)S(1)}) all-reduce(f32[10]{0:T(128)S(1)} %get-tuple-element.28, f32[10]{0:T(128)S(1)} %get-tuple-element.27), channel_id=1, replica_groups=mesh['rows'=8,'vecs'=4] {'rows'}, use_global_device_ids=true, to_apply=%region_5.6 | all-reduce | flops 20 | bytes 160 | tf_op jit(solution)/shard_map/psum | solution.py:48
  394.0 0.5 rsqrt_multiply_fusion
  394.5 5.5 %subtract_convert_fusion = bf16[10,65536]{1,0:T(8,128)(2,1)} fusion(f32[10,65536]{1,0:T(8,128)} %copy.32, bf16[10,65536]{1,0:T(8,128)(2,1)} %bitcast.42, f32[10]{0:T(128)S(1)} %copy-done.17, f32[65536]{0:T(1024)S(1)} %copy-done.3, f32[65536]{0:T(1024)S(1)} %copy-done.5, f32[10]{0:T(128)S(1)} %copy-done.16, f32[65536]{0:T(1024)S(1)} %copy-done.7, ...), kind=kLoop, calls=%fused_computation.19 | loop fusion | flops 5898240 | bytes 6029432 | tf_op jit(solution)/shard_map/convert_element_type | solution.py:86
  400.1 0.0 copy-done.1
  (31 shorter events, 0.1 us)
Async XLA Ops:
  0.6 67.4 %copy-start = (bf16[100,40]{0,1:T(8,128)(2,1)S(1)}, bf16[100,40]{0,1:T(8,128)(2,1)}, u32[]{:S(2)}) copy-start(bf16[100,40]{0,1:T(8,128)(2,1)} %param.14) | copy-start | bytes 24004
  10.8 5.0 %copy-start.19 = (s32[1,4096]{1,0:T(1,128)S(1)}, s32[1,4096]{1,0:T(1,128)}, u32[]{:S(2)}) copy-start(s32[1,4096]{1,0:T(1,128)} %param.21) | copy-start | bytes 49156
  10.8 10.3 %copy-start.2 = (f32[65536]{0:T(1024)S(1)}, f32[65536]{0:T(1024)}, u32[]{:S(2)}) copy-start(f32[65536]{0:T(1024)} %param.16) | copy-start | bytes 786436
  10.8 11.1 %copy-start.4 = (f32[65536]{0:T(1024)S(1)}, f32[65536]{0:T(1024)}, u32[]{:S(2)}) copy-start(f32[65536]{0:T(1024)} %param.17) | copy-start | bytes 786436
  10.8 12.0 %copy-start.6 = (f32[65536]{0:T(1024)S(1)}, f32[65536]{0:T(1024)}, u32[]{:S(2)}) copy-start(f32[65536]{0:T(1024)} %param.18) | copy-start | bytes 786436
  10.8 13.4 %copy-start.15 = (f32[10]{0:T(128)S(1)}, f32[10]{0:T(128)}, u32[]{:S(2)}) copy-start(f32[10]{0:T(128)} %param.15) | copy-start | bytes 124
  10.8 13.9 %copy-start.14 = (s32[1,4096]{1,0:T(1,128)S(1)}, s32[1,4096]{1,0:T(1,128)}, u32[]{:S(2)}) copy-start(s32[1,4096]{1,0:T(1,128)} %param.20) | copy-start | bytes 49156
  10.8 53.9 %all-to-all-start = ((bf16[25,4,16384]{2,0,1:T(8,128)(2,1)}), bf16[25,4,16384]{2,0,1:T(8,128)(2,1)}, u32[]{:S(2)}, u32[]{:S(2)}) async-start(bf16[25,4,16384]{2,0,1:T(8,128)(2,1)} %copy.25), calls=%async_computation | async-start | bytes 8388608 | tf_op jit(solution)/shard_map/all_to_all | solution.py:42
  15.8 60.9 %collective-permute-start = (s32[1,4096]{1,0:T(1,128)S(1)}, s32[1,4096]{1,0:T(1,128)S(1)}, u32[]{:S(2)}, u32[]{:S(2)}) collective-permute-start(s32[1,4096]{1,0:T(1,128)S(1)} %copy-done.19), channel_id=1, source_target_pairs={{0,4},{4,8},{8,12},{12,16},{16,20},{20,24},{24,28},{28,0},{1,5},{5... | collective-permute-start | bytes 49160 | tf_op jit(solution)/shard_map/ppermute | solution.py:12
  18.9 6.5 %collective-permute-start.2 = (s32[1]{0:T(128)}, s32[1]{0:T(128)}, u32[]{:S(2)}, u32[]{:S(2)}) collective-permute-start(s32[1]{0:T(128)} %param.19), channel_id=1, source_target_pairs={{0,4},{4,8},{8,12},{12,16},{16,20},{20,24},{24,28},{28,0},{1,5},{5... | collective-permute-start | bytes 20 | tf_op jit(solution)/shard_map/ppermute | solution.py:12
  24.8 0.6 copy-start.10
  73.1 29.2 %all-to-all-start.1 = ((bf16[4,10,16384]{2,1,0:T(8,128)(2,1)}), bf16[4,10,16384]{2,1,0:T(8,128)(2,1)S(1)}, u32[]{:S(2)}, u32[]{:S(2)}) async-start(bf16[4,10,16384]{2,1,0:T(8,128)(2,1)} %all_to_all.34), calls=%async_computation.1 | async-start | bytes 4194304 | tf_op jit(solution)/shard_map/all_to_all | solution.py:46
  76.8 36.6 %copy-start.11 = (s32[4096,1]{0,1:T(1,128)}, s32[4096,1]{0,1:T(1,128)S(1)}, u32[]{:S(2)}) copy-start(s32[4096,1]{0,1:T(1,128)S(1)} %compare_select_fusion.1) | copy-start | bytes 49156
  113.3 36.4 %copy-start.13 = (pred[4096]{0:T(1024)(128)(4,1)S(1)}, pred[4096]{0:T(1024)(128)(4,1)}, u32[]{:S(2)}) copy-start(pred[4096]{0:T(1024)(128)(4,1)} %iota_compare_fusion) | copy-start | bytes 12292
  134.8 45.6 %collective-permute-start.1 = (bf16[10,4096]{1,0:T(8,128)(2,1)S(1)}, bf16[10,4096]{1,0:T(8,128)(2,1)}, u32[]{:S(2)}, u32[]{:S(2)}) collective-permute-start(bf16[10,4096]{1,0:T(8,128)(2,1)S(1)} %copy.28), channel_id=1, source_target_pairs={{0,4},{4,8},{8,12},{12,16},{16,20},{20,24},{24,28},{28,0},{1,5},{5... | collective-permute-start | bytes 245768 | tf_op jit(solution)/shard_map/ppermute | solution.py:12
  174.1 45.4 %collective-permute-start.3 = (bf16[10,4096]{1,0:T(8,128)(2,1)}, bf16[10,4096]{1,0:T(8,128)(2,1)}, u32[]{:S(2)}, u32[]{:S(2)}) collective-permute-start(bf16[10,4096]{1,0:T(8,128)(2,1)} %copy.30), channel_id=1, source_target_pairs={{0,28},{4,0},{8,4},{12,8},{16,12},{20,16},{24,20},{28,24},{1,29},{... | collective-permute-start | bytes 245768 | tf_op jit(solution)/shard_map/ppermute | solution.py:12
  220.4 29.1 %copy-start.12 = (pred[4096]{0:T(1024)(128)(4,1)S(1)}, pred[4096]{0:T(1024)(128)(4,1)}, u32[]{:S(2)}) copy-start(pred[4096]{0:T(1024)(128)(4,1)} %get-tuple-element.36) | copy-start | bytes 12292
  351.5 19.5 %copy-start.8 = (f32[4,16384]{1,0:T(4,128)S(1)}, f32[4,16384]{1,0:T(4,128)}, u32[]{:S(2)}) copy-start(f32[4,16384]{1,0:T(4,128)} %add.124) | copy-start | bytes 786436
  351.5 19.5 %copy-start.9 = (f32[4,16384]{1,0:T(4,128)S(1)}, f32[4,16384]{1,0:T(4,128)}, u32[]{:S(2)}) copy-start(f32[4,16384]{1,0:T(4,128)} %mul.101) | copy-start | bytes 786436
  351.5 19.5 %copy-start.16 = (f32[10]{0:T(128)S(1)}, f32[10]{0:T(128)}, u32[]{:S(2)}) copy-start(f32[10]{0:T(128)} %param.15) | copy-start | bytes 124
  351.5 19.5 %copy-start.17 = (f32[10]{0:T(128)S(1)}, f32[10]{0:T(128)}, u32[]{:S(2)}) copy-start(f32[10]{0:T(128)} %get-tuple-element.33) | copy-start | bytes 124
  351.6 19.5 %copy-start.18 = (f32[10]{0:T(128)S(1)}, f32[10]{0:T(128)}, u32[]{:S(2)}) copy-start(f32[10]{0:T(128)} %get-tuple-element.34) | copy-start | bytes 124
  371.0 23.5 %copy-start.3 = (f32[65536]{0:T(1024)S(1)}, f32[65536]{0:T(1024)}, u32[]{:S(2)}) copy-start(f32[65536]{0:T(1024)} %param.16) | copy-start | bytes 786436
  371.0 23.5 %copy-start.5 = (f32[65536]{0:T(1024)S(1)}, f32[65536]{0:T(1024)}, u32[]{:S(2)}) copy-start(f32[65536]{0:T(1024)} %param.17) | copy-start | bytes 786436
  371.0 23.5 %copy-start.7 = (f32[65536]{0:T(1024)S(1)}, f32[65536]{0:T(1024)}, u32[]{:S(2)}) copy-start(f32[65536]{0:T(1024)} %param.18) | copy-start | bytes 786436
  394.5 5.6 %copy-start.1 = (bf16[100,40]{0,1:T(8,128)(2,1)S(1)}, bf16[100,40]{0,1:T(8,128)(2,1)}, u32[]{:S(2)}) copy-start(bf16[100,40]{0,1:T(8,128)(2,1)} %param.14) | copy-start | bytes 24004
where the time goes:
time: 401 us; the launch traced here: 400 us
  other arithmetic  169 us (42%)
  local copies, waits for them, and re-layouts  126 us (31%)
  waiting for transfers between devices  63.7 us (16%)
  blocking collectives  19.1 us (5%)
  starting transfers between devices  18.8 us (5%)
    add x1, other arithmetic, on_device(): total_coupled = (neighbour_sum + link_sum).reshape(vector_part, rows_local)  82.5 us
    reshape x2, local copies, waits for them, and re-layouts, on_device(): total_coupled = (neighbour_sum + link_sum).reshape(vector_part, rows_local)  38.9 us
    all_to_all x1, waiting for transfers between devices, on_device(): lax.all_to_all(basis, 'vecs', split_axis=1, concat_axis=0, tiled=True)  38.1 us
    all_to_all x1, waiting for transfers between devices, on_device(): lax.all_to_all(quarter_vecs, 'vecs', split_axis=0, concat_axis=1, tiled=T...  25.6 us
    scatter-add x1, other arithmetic, on_device(): link_last = jnp.zeros((vector_part, plane_cells), jnp.float32).at[:, lowe...  24.1 us
    scatter-add x1, other arithmetic, on_device(): link_first = jnp.zeros((vector_part, plane_cells), jnp.float32).at[:, dow...  24.1 us
    psum x1, blocking collectives, on_device(): vector_sq = lax.psum(jnp.sum(vectors * vectors, axis=1), 'rows')  19.1 us
    convert_element_type x1, other arithmetic, on_device(): vectors = eigvecs.astype(jnp.float32)  18.2 us
  transfers between devices with their start and end apart: 6, of which 2 were waited for; matrix products, arithmetic and copies ran while one was open for 21% of the time, Pallas kernels for 0%

commit v1 on v0

v1 whole, which is shorter than its diff:
```python
import functools

import jax
import jax.numpy as jnp
from jax import lax
from jax.experimental import pallas as pl
from jax.experimental.pallas import tpu as pltpu
from jax.sharding import PartitionSpec as P

WID = 64
LANES = 128
PAD = 16
BLOCK = 512
FULL = 8


def remote(src, dst, send_sem, recv_sem, where):
    return pltpu.make_async_remote_copy(
        src_ref=src,
        dst_ref=dst,
        send_sem=send_sem,
        recv_sem=recv_sem,
        device_id=where,
        device_id_type=pl.DeviceIdType.MESH,
    )


def kernel(
    count,
    planes,
    cells,
    vector_part,
    basis,
    factors,
    eigen,
    stiffness,
    damping,
    mass,
    links,
    eig_out,
    res_out,
    norm_out,
    own_basis,
    mate_basis,
    wire_out,
    wire_in,
    values,
    face_out,
    face_in,
    links_in,
    link_sums,
    link_part,
    stat_out,
    stat_in,
    local_sem,
    mate_send,
    mate_recv,
    wire_send,
    wire_recv,
    face_send,
    face_recv,
    stat_send,
    stat_recv,
):
    row = lax.axis_index("rows")
    vec = lax.axis_index("vecs")
    mate = {"vecs": vec + 1 - 2 * (vec % 2)}
    across = {"vecs": (vec + 2) % 4}
    above = {"rows": (row + 1) % count}
    below = {"rows": (row + count - 1) % count}
    half = cells // 2
    eighth = cells // 8
    slots = links.shape[1]

    def plane_at(step):
        return (step + planes - 1) % planes

    def lanes_of(plane):
        return pl.ds(pl.multiple_of(plane * cells, cells), cells)

    def local_copy(plane):
        return pltpu.make_async_copy(
            basis.at[:, lanes_of(plane)], own_basis.at[:, lanes_of(plane)], local_sem.at[plane]
        )

    def mate_copy(plane):
        return remote(
            basis.at[:, lanes_of(plane)],
            mate_basis.at[:, lanes_of(plane)],
            mate_send.at[plane],
            mate_recv.at[plane],
            mate,
        )

    def wire_copy(plane):
        return remote(
            wire_out.at[plane], wire_in.at[plane], wire_send.at[plane], wire_recv.at[plane], across
        )

    def face_copy(which):
        return remote(
            face_out.at[which],
            face_in.at[which],
            face_send.at[which],
            face_recv.at[which],
            above if which == 0 else below,
        )

    def links_copy():
        return remote(links, links_in, face_send.at[2], face_recv.at[2], above)

    def stat_copy(step):
        return remote(
            stat_out,
            stat_in.at[step],
            stat_send.at[step],
            stat_recv.at[step],
            {"rows": (row + step) % count},
        )

    def each(first, last, body):
        def run(step, carry):
            body(step)
            return carry

        lax.fori_loop(first, last, run, 0)

    each(0, planes, lambda step: local_copy(plane_at(step)).start())

    barrier = pltpu.get_barrier_semaphore()

    def greet(where):
        pl.semaphore_signal(barrier, inc=1, device_id=where, device_id_type=pl.DeviceIdType.MESH)

    greet(mate)
    greet(across)
    each(1, count, lambda step: greet({"rows": (row + step) % count}))
    pl.semaphore_wait(barrier, count + 1)

    each(0, planes, lambda step: mate_copy(plane_at(step)).start())
    links_copy().start()

    values[...] = jnp.zeros_like(values)
    row_iota = lax.broadcasted_iota(jnp.int32, (FULL, eighth), 0)
    rest = row_iota < vector_part - FULL

    def produce(step):
        plane = plane_at(step)
        local_copy(plane).wait()
        mate_copy(plane).wait_recv()
        both = jnp.dot(
            factors[0], own_basis[:, lanes_of(plane)], preferred_element_type=jnp.float32
        ) + jnp.dot(factors[1], mate_basis[:, lanes_of(plane)], preferred_element_type=jnp.float32)
        values[plane + 1, :, LANES : LANES + cells] = both[:PAD]
        top = both[PAD : PAD + FULL]
        tail = both[PAD + FULL :]
        wire_out[plane, :, :half] = jnp.concatenate([top[:, :half], top[:, half:]], axis=0).astype(
            jnp.bfloat16
        )
        packed = []
        for side in range(2):
            total = None
            for part in range(4):
                start = (4 * side + part) * eighth
                piece = tail[:, start : start + eighth]
                if part:
                    piece = pltpu.roll(piece, 2 * part, 0)
                total = piece if total is None else total + piece
            packed.append(total)
        wire_out[plane, :, half:] = jnp.concatenate(packed, axis=0).astype(jnp.bfloat16)
        wire_copy(plane).start()

    each(0, planes, produce)

    stat_out[...] = jnp.zeros_like(stat_out)

    def fold(block):
        total = block[:, :LANES]
        for start in range(LANES, block.shape[1], LANES):
            total = total + block[:, start : start + LANES]
        return total

    def finish(plane):
        wire_copy(plane).wait_recv()
        squares = jnp.zeros((PAD, LANES), jnp.float32)
        for part in range(8):
            side = part // 4
            lanes = slice(LANES + part * eighth, LANES + (part + 1) * eighth)
            inner = (part % 4) * eighth
            top = wire_in[plane, :, inner : inner + eighth].astype(jnp.float32)
            top = top[side * FULL : (side + 1) * FULL]
            tail = wire_in[plane, :, half:].astype(jnp.float32)
            tail = tail[side * FULL : (side + 1) * FULL]
            if part % 4:
                tail = pltpu.roll(tail, FULL - 2 * (part % 4), 0)
            tail = jnp.where(rest, tail, 0.0)
            held = values[plane + 1, :, lanes] + jnp.concatenate([top, tail], axis=0)
            rounded = held.astype(jnp.bfloat16)
            exact = rounded.astype(jnp.float32)
            values[plane + 1, :, lanes] = exact
            start = pl.multiple_of(plane * cells + part * eighth, eighth)
            eig_out[:, pl.ds(start, eighth)] = rounded[:vector_part]
            squares = squares + fold(exact * exact)
        stat_out[:PAD] += squares

    lam = eigen[...]
    lam_b = jnp.broadcast_to(lam, (PAD, LANES))
    lam_sq = jnp.tile(lam_b * lam_b, (1, BLOCK // LANES))
    lam_b = jnp.tile(lam_b, (1, BLOCK // LANES))
    coupling = lam_sq * 0.1 + lam_b * 0.3 + 1.0
    column = lax.broadcasted_iota(jnp.int32, (PAD, BLOCK), 1) % WID
    wide = BLOCK + 2 * LANES

    def stencil(plane, link):
        squares = jnp.zeros((PAD, LANES), jnp.float32)
        for start in range(0, cells, BLOCK):
            inner = slice(LANES + start, LANES + start + BLOCK)
            around = values[plane + 1, :, start : start + wide]
            mid = around[:, LANES : LANES + BLOCK]

            def moved(amount):
                return pltpu.roll(around, amount % wide, 1)[:, LANES : LANES + BLOCK]

            total = values[plane, :, inner] + values[plane + 2, :, inner]
            total = total + (moved(WID) + moved(-WID))
            total = total + jnp.where(column < WID - 1, moved(-1), 0.0)
            total = total + jnp.where(column > 0, moved(1), 0.0)
            if link is not None:
                total = total + link_sums[link, :, start : start + BLOCK]
            at = pl.ds(pl.multiple_of(plane * cells + start, BLOCK), BLOCK)
            diagonal = lam_sq * mass[:, at] + lam_b * damping[:, at] + stiffness[:, at]
            full = diagonal * mid - coupling * total
            res_out[:, at] = full.astype(jnp.bfloat16)[:vector_part]
            squares = squares + fold(full * full)
        stat_out[PAD:] += squares

    tiles = cells // LANES

    def link_side(which, lists, source_row, target_row):
        stacked = jnp.concatenate(
            [face_in[which, :, t * LANES : (t + 1) * LANES] for t in range(tiles)], axis=0
        )
        link_part[...] = jnp.zeros_like(link_part)
        low_iota = lax.broadcasted_iota(jnp.int32, (LANES, BLOCK), 0)

        def some(step):
            at = pl.ds(pl.multiple_of(step * BLOCK, BLOCK), BLOCK)
            source = lists[source_row : source_row + 1, at]
            target = lists[target_row : target_row + 1, at]
            low = jnp.where(low_iota == source % LANES, 1.0, 0.0).astype(jnp.bfloat16)
            picked = jnp.dot(stacked, low, preferred_element_type=jnp.float32)
            high = jnp.broadcast_to(source // LANES, (PAD, BLOCK))
            got = jnp.zeros((PAD, BLOCK), jnp.float32)
            for t in range(tiles):
                got = got + jnp.where(high == t, picked[t * PAD : (t + 1) * PAD], 0.0)
            high = jnp.broadcast_to(target // LANES, (PAD, BLOCK))
            spread = jnp.concatenate(
                [jnp.where(high == t, got, 0.0).astype(jnp.bfloat16) for t in range(tiles)], axis=0
            )
            low = jnp.where(low_iota == target % LANES, 1.0, 0.0).astype(jnp.bfloat16)
            link_part[...] += lax.dot_general(
                spread, low, (((1,), (1,)), ((), ())), preferred_element_type=jnp.float32
            )

        each(0, slots // BLOCK, some)
        for t in range(tiles):
            link_sums[which, :, t * LANES : (t + 1) * LANES] = link_part[t * PAD : (t + 1) * PAD]

    def send_face(which, plane):
        face_out[which] = values[plane + 1, :, LANES : LANES + cells].astype(jnp.bfloat16)
        face_copy(which).start()

    finish(planes - 1)
    send_face(0, planes - 1)
    finish(0)
    send_face(1, 0)
    finish(1)

    def advance(plane):
        finish(plane)
        stencil(plane - 1, None)

    middle = max(2, planes // 2 - 1)
    each(2, middle, advance)
    face_copy(0).wait_recv()
    links_copy().wait_recv()
    link_side(0, links_in, 0, 1)
    face_copy(1).wait_recv()
    link_side(1, links, 1, 0)
    stencil(0, 0)
    each(middle, planes - 1, advance)
    stencil(planes - 2, None)
    stencil(planes - 1, 1)

    each(1, count, lambda step: stat_copy(step).start())
    stat_in[0] = stat_out[...]
    each(1, count, lambda step: stat_copy(step).wait_recv())
    total = stat_in[0]
    for step in range(1, count):
        total = total + stat_in[step]
    sums = jnp.sum(total, axis=1, keepdims=True)
    norms = jnp.sqrt(sums[PAD:]) / jnp.sqrt(sums[:PAD] + 1.0)
    norm_out[...] = jnp.broadcast_to(norms, norm_out.shape)

    each(0, planes, lambda plane: mate_copy(plane).wait_send())
    each(0, planes, lambda plane: wire_copy(plane).wait_send())
    links_copy().wait_send()
    face_copy(0).wait_send()
    face_copy(1).wait_send()
    each(1, count, lambda step: stat_copy(step).wait_send())


def on_device(
    basis,
    coefficients,
    eigen_values,
    stiffness,
    damping,
    mass,
    link_count,
    lower_cells,
    upper_cells,
):
    count = lax.axis_size("rows")
    vec = lax.axis_index("vecs")
    vector_part = eigen_values.shape[0]
    rank_part, rows_local = basis.shape
    cells = WID * WID
    planes = rows_local // cells
    slots = lower_cells.shape[1]
    mate = vec + 1 - 2 * (vec % 2)
    across = (vec + 2) % 4

    def factor(rank_owner, vector_owner):
        piece = lax.dynamic_slice(
            coefficients,
            (rank_owner * rank_part, vector_owner * vector_part),
            (rank_part, vector_part),
        )
        return jnp.pad(piece.T, ((0, PAD - vector_part), (0, 0)))

    factors = jnp.stack(
        [
            jnp.concatenate([factor(owner, vec), factor(owner, across)], axis=0)
            for owner in (vec, mate)
        ]
    )
    eigen = jnp.pad(eigen_values, (0, PAD - vector_part))[:, None]
    used = jnp.arange(slots, dtype=jnp.int32) < link_count[0]
    links = jnp.where(used[None, :], jnp.concatenate([lower_cells, upper_cells]), -1)
    links = jnp.pad(links, ((0, 6), (0, 0)), constant_values=-1)
    vmem = pl.BlockSpec(memory_space=pltpu.VMEM)
    wire = cells // 2 + cells // 8
    dma = pltpu.SemaphoreType.DMA
    eigvecs, residuals, norms = pl.pallas_call(
        functools.partial(kernel, count, planes, cells, vector_part),
        out_shape=(
            jax.ShapeDtypeStruct((vector_part, rows_local), jnp.bfloat16),
            jax.ShapeDtypeStruct((vector_part, rows_local), jnp.bfloat16),
            jax.ShapeDtypeStruct((PAD, LANES), jnp.float32),
        ),
        in_specs=[pl.BlockSpec(memory_space=pl.ANY)] + [vmem] * 6,
        out_specs=(vmem, vmem, vmem),
        scratch_shapes=[
            pltpu.VMEM((rank_part, rows_local), jnp.bfloat16),
            pltpu.VMEM((rank_part, rows_local), jnp.bfloat16),
            pltpu.VMEM((planes, PAD, wire), jnp.bfloat16),
            pltpu.VMEM((planes, PAD, wire), jnp.bfloat16),
            pltpu.VMEM((planes + 2, PAD, cells + 2 * LANES), jnp.float32),
            pltpu.VMEM((2, PAD, cells), jnp.bfloat16),
            pltpu.VMEM((2, PAD, cells), jnp.bfloat16),
            pltpu.VMEM((8, slots), jnp.int32),
            pltpu.VMEM((2, PAD, cells), jnp.float32),
            pltpu.VMEM((cells // LANES * PAD, LANES), jnp.float32),
            pltpu.VMEM((2 * PAD, LANES), jnp.float32),
            pltpu.VMEM((count, 2 * PAD, LANES), jnp.float32),
            dma((planes,)),
            dma((planes,)),
            dma((planes,)),
            dma((planes,)),
            dma((planes,)),
            dma((3,)),
            dma((3,)),
            dma((count,)),
            dma((count,)),
        ],
        compiler_params=pltpu.CompilerParams(
            collective_id=0, has_side_effects=True, vmem_limit_bytes=56 * 1024 * 1024
        ),
    )(
        basis,
        factors,
        eigen,
        stiffness[None, :],
        damping[None, :],
        mass[None, :],
        links,
    )
    return eigvecs, residuals, norms[:vector_part, 0]


def solution(mesh):
    placed = (
        P("vecs", "rows"),
        P(),
        P("vecs"),
        P("rows"),
        P("rows"),
        P("rows"),
        P("rows"),
        P("rows", None),
        P("rows", None),
    )
    return jax.shard_map(
        on_device,
        mesh=mesh,
        in_specs=placed,
        out_specs=(P("vecs", "rows"), P("vecs", "rows"), P("vecs")),
        check_vma=False,
    )
```

time: 401 us -> 59.1 us (0.15)
  other arithmetic: 169 us -> 1.41 us
  local copies, waits for them, and re-layouts: 126 us -> 8.76 us
  waiting for transfers between devices: 63.7 us -> 0 us
  Pallas kernels: 0 us -> 47.1 us
  blocking collectives: 19.1 us -> 0 us
  starting transfers between devices: 18.8 us -> 0 us
    add x2 -> x0, other arithmetic: 83.1 us -> none  [the longest x1 82.5 us: on_device(): total_coupled = (neighbour_sum + link_sum).reshape(vector_part, rows_local)]
    all_to_all x2 -> x0, waiting for transfers between devices: 63.7 us -> none  [the longest x1 38.1 us: on_device(): lax.all_to_all(basis, 'vecs', split_axis=1, concat_axis=0, tiled=True)]
    scatter-add x2 -> x0, other arithmetic: 48.2 us -> none  [the longest x1 24.1 us: on_device(): link_last = jnp.zeros((vector_part, plane_cells), jnp.float32).at[:, lowe...]
    pallas_call x0 -> x1, Pallas kernels: none -> 47.1 us  [on_device(): pl.pallas_call(functools.partial(kernel, count, planes, cells, vector_par...]
    reshape x2 -> x0, local copies, waits for them, and re-layouts: 38.9 us -> none  [on_device(): total_coupled = (neighbour_sum + link_sum).reshape(vector_part, rows_local)]
    all_to_all x6 -> x0, local copies, waits for them, and re-layouts: 28.6 us -> none  [the longest x3 15.1 us: on_device(): lax.all_to_all(quarter_vecs, 'vecs', split_axis=0, concat_axis=1, tiled=T...]
    gather x2 -> x0, local copies, waits for them, and re-layouts: 27.4 us -> none  [the longest x1 15 us: on_device(): last_plane[:, lower_cells[0]]]
    convert_element_type x4 -> x0, other arithmetic: 25.6 us -> none  [the longest x1 18.2 us: on_device(): vectors = eigvecs.astype(jnp.float32)]
  transfers between devices with their start and end apart: 6 -> 0, of which waited for: 2 -> 0; matrix products, arithmetic and copies ran while one was open for 21% -> 0% of each run, Pallas kernels for 0% -> 0%
where the time goes in v1:
time: 59.1 us; the launch traced here: 58.6 us
  Pallas kernels  47.1 us (80%)
  local copies, waits for them, and re-layouts  8.76 us (15%)
  other arithmetic  1.41 us (2%)
  between operations  1.33 us (2%)
    pallas_call x1, Pallas kernels, on_device(): pl.pallas_call(functools.partial(kernel, count, planes, cells, vector_par...  47.1 us
    unnamed x4, local copies, waits for them, and re-layouts  4.52 us
    broadcast_in_dim x2, local copies, waits for them, and re-layouts, on_device(): eigen = jnp.pad(eigen_values, (0, PAD - vector_part))[:, None]  1.34 us
    slice x1, local copies, waits for them, and re-layouts, on_device(): return (eigvecs, residuals, norms[:vector_part, 0])  1.32 us

profile of v1, /device:TPU:0, one launch (start us, length us, event | category | flops | bytes accessed | tf_op | source)
XLA Modules:
  0.0 58.6 jit_solution(16651586481836225697)
XLA Ops:
  1.3 0.7 %pad_bitcast_fusion = f32[16,1]{0,1:T(1,128)S(1)} fusion(f32[10]{0:T(128)} %param.11), kind=kLoop, calls=%fused_computation.18 | loop fusion | bytes 104 | tf_op jit(solution)/shard_map/broadcast_in_dim | solution.py:348
  2.0 0.7 %copy.13.eigen = f32[16,1]{1,0:T(8,128)} copy(f32[16,1]{0,1:T(1,128)S(1)} %pad_bitcast_fusion) | data formatting | bytes 128 | tf_op jit(solution)/shard_map/broadcast_in_dim | solution.py:348
  2.7 0.9 %dynamic-slice_bitcast_fusion.3 = (bf16[10,25]{1,0:T(8,128)(2,1)S(1)}, bf16[10,25]{1,0:T(8,128)(2,1)S(1)}, bf16[10,25]{1,0:T(8,128)(2,1)S(1)}, bf16[10,25]{1,0:T(8,128)(2,1)S(1)}) fusion(bf16[100,40]{0,1:T(8,128)(2,1)} %param.10, s32[]{:T(128)S(6)} %select_n.31, s32[]{:T(128)S(6)} %select_n.32, s32[]{:T(128)S(6)} %select_n.34, s32[]{:T(128)S(6)} %select_n.36), kind=kLoop, calls=%fused_computation.17 | loop fusion | bytes 4016 | tf_op jit(solution)/shard_map/transpose | solution.py:340
  3.6 0.6 %pad_maximum_fusion.factors = bf16[2,32,25]{2,1,0:T(8,128)(2,1)} fusion(bf16[1,32,25]{2,1,0:T(8,128)(2,1)S(1)} %get-tuple-element.14, bf16[1,32,25]{2,1,0:T(8,128)(2,1)S(1)} %get-tuple-element.13), kind=kLoop, calls=%fused_computation.7 | loop fusion | flops 1600 | bytes 6400 | tf_op jit(solution)/shard_map/stack | solution.py:342
  4.2 0.8 %add_select_fusion = s32[2,4096]{1,0:T(2,128)S(1)} fusion(s32[1,4096]{1,0:T(1,128)} %param.17, s32[1,4096]{1,0:T(1,128)} %param.16, pred[4096]{0:T(1024)(128)(4,1)S(1)} %iota_compare_fusion.2), kind=kLoop, calls=%fused_computation | loop fusion | flops 16384 | bytes 69632 | tf_op jit(solution)/shard_map/jit(_where)/select_n | solution.py:350
  5.0 0.7 %pad.26.links = s32[8,4096]{1,0:T(8,128)} pad(s32[2,4096]{1,0:T(2,128)S(1)} %add_select_fusion, s32[]{:T(128)} %constant.42.clone.1), padding=0_6x0_0 | pad | bytes 163844 | tf_op jit(solution)/shard_map/jit(_pad)/pad | solution.py:351
  5.6 47.1 %shard_map.112 = (bf16[10,65536]{1,0:T(8,128)(2,1)}, bf16[10,65536]{1,0:T(8,128)(2,1)}, f32[16,128]{1,0:T(8,128)}) custom-call(bf16[25,65536]{1,0:T(8,128)(2,1)} %basis.1, bf16[2,32,25]{2,1,0:T(8,128)(2,1)} %pad_maximum_fusion.factors, f32[16,1]{1,0:T(8,128)} %copy.13.eigen, f32[1,65536]{1,0:T(1,128)} %bitcast.19, f32[1,65536]{1,0:T(1,128)} %bitcast.20, ...), custom_call_target="tpu_custom_call" | custom-call | tf_op jit(solution)/shard_map/pallas_call | solution.py:355
  52.7 1.3 %slice_reduce_fusion = f32[10]{0:T(128)} fusion(f32[16,128]{1,0:T(8,128)} %get-tuple-element.8), kind=kLoop, calls=%fused_computation.13 | loop fusion | bytes 80 | tf_op jit(solution)/shard_map/slice | solution.py:399
  54.0 0.0 copy-start
  54.0 3.2 %copy.17 = bf16[10,65536]{1,0:T(8,128)(2,1)} copy(bf16[10,65536]{1,0:T(8,128)(2,1)} %get-tuple-element.18) | data formatting | bytes 2621440
  57.2 0.0 copy-done
  57.2 1.3 %copy.18 = bf16[10,65536]{1,0:T(8,128)(2,1)} copy(bf16[10,65536]{1,0:T(8,128)(2,1)S(1)} %copy-done) | data formatting | bytes 2621440
  (2 shorter events, 0.0 us)
Async XLA Ops:
  54.0 3.2 %copy-start = (bf16[10,65536]{1,0:T(8,128)(2,1)S(1)}, bf16[10,65536]{1,0:T(8,128)(2,1)}, u32[]{:S(2)}) copy-start(bf16[10,65536]{1,0:T(8,128)(2,1)} %get-tuple-element.19) | copy-start | bytes 3932164

commit v2 on v1

--- a/solution.py
+++ b/solution.py
@@ -31,12 +31,14 @@
     cells,
     vector_part,
     basis,
-    factors,
+    coefficients,
     eigen,
     stiffness,
     damping,
     mass,
-    links,
+    used,
+    lower,
+    upper,
     eig_out,
     res_out,
     norm_out,
@@ -52,6 +54,8 @@
     link_part,
     stat_out,
     stat_in,
+    links,
+    factors,
     local_sem,
     mate_send,
     mate_recv,
@@ -71,6 +75,7 @@
     half = cells // 2
     eighth = cells // 8
     slots = links.shape[1]
+    rank_part = basis.shape[0]
 
     def plane_at(step):
         return (step + planes - 1) % planes
@@ -135,12 +140,36 @@
     greet(mate)
     greet(across)
     each(1, count, lambda step: greet({"rows": (row + step) % count}))
+
+    slot = lax.broadcasted_iota(jnp.int32, (1, slots), 1)
+    is_used = slot < used[0]
+    links[...] = jnp.full_like(links, -1)
+    links[0:1] = jnp.where(is_used, lower[...], -1)
+    links[1:2] = jnp.where(is_used, upper[...], -1)
+
+    total_vectors, total_rank = coefficients.shape
+    place = lax.broadcasted_iota(jnp.int32, (2 * PAD, total_vectors), 0)
+    vector = lax.broadcasted_iota(jnp.int32, (2 * PAD, total_vectors), 1)
+    owner = jnp.where(place < PAD, vec, (vec + 2) % 4)
+    inside = place % PAD
+    choose = (inside < vector_part) & (vector == owner * vector_part + inside)
+    choose = jnp.where(choose, 1.0, 0.0).astype(jnp.bfloat16)
+    chosen = jnp.dot(choose, coefficients[...], preferred_element_type=jnp.float32)
+    chosen = chosen.astype(jnp.bfloat16)
+    rank = lax.broadcasted_iota(jnp.int32, (total_rank, rank_part), 0)
+    own_rank = lax.broadcasted_iota(jnp.int32, (total_rank, rank_part), 1)
+    for side, source in enumerate((vec, vec + 1 - 2 * (vec % 2))):
+        pick = jnp.where(rank == source * rank_part + own_rank, 1.0, 0.0).astype(jnp.bfloat16)
+        part = jnp.dot(chosen, pick, preferred_element_type=jnp.float32)
+        factors[side] = part.astype(jnp.bfloat16)
+
+    values[...] = jnp.zeros_like(values)
+    stat_out[...] = jnp.zeros_like(stat_out)
     pl.semaphore_wait(barrier, count + 1)
 
     each(0, planes, lambda step: mate_copy(plane_at(step)).start())
     links_copy().start()
 
-    values[...] = jnp.zeros_like(values)
     row_iota = lax.broadcasted_iota(jnp.int32, (FULL, eighth), 0)
     rest = row_iota < vector_part - FULL
 
@@ -171,8 +200,6 @@
         wire_copy(plane).start()
 
     each(0, planes, produce)
-
-    stat_out[...] = jnp.zeros_like(stat_out)
 
     def fold(block):
         total = block[:, :LANES]
@@ -203,7 +230,11 @@
             squares = squares + fold(exact * exact)
         stat_out[:PAD] += squares
 
-    lam = eigen[...]
+    diag = lax.broadcasted_iota(jnp.int32, (PAD, vector_part), 0) == lax.broadcasted_iota(
+        jnp.int32, (PAD, vector_part), 1
+    )
+    lam = jnp.where(diag, jnp.broadcast_to(eigen[...], (PAD, vector_part)), 0.0)
+    lam = jnp.sum(lam, axis=1, keepdims=True)
     lam_b = jnp.broadcast_to(lam, (PAD, LANES))
     lam_sq = jnp.tile(lam_b * lam_b, (1, BLOCK // LANES))
     lam_b = jnp.tile(lam_b, (1, BLOCK // LANES))
@@ -247,17 +278,17 @@
             at = pl.ds(pl.multiple_of(step * BLOCK, BLOCK), BLOCK)
             source = lists[source_row : source_row + 1, at]
             target = lists[target_row : target_row + 1, at]
-            low = jnp.where(low_iota == source % LANES, 1.0, 0.0).astype(jnp.bfloat16)
+            low = jnp.where(low_iota == (source & (LANES - 1)), 1.0, 0.0).astype(jnp.bfloat16)
             picked = jnp.dot(stacked, low, preferred_element_type=jnp.float32)
-            high = jnp.broadcast_to(source // LANES, (PAD, BLOCK))
+            high = jnp.broadcast_to(source >> 7, (PAD, BLOCK))
             got = jnp.zeros((PAD, BLOCK), jnp.float32)
             for t in range(tiles):
                 got = got + jnp.where(high == t, picked[t * PAD : (t + 1) * PAD], 0.0)
-            high = jnp.broadcast_to(target // LANES, (PAD, BLOCK))
+            high = jnp.broadcast_to(target >> 7, (PAD, BLOCK))
             spread = jnp.concatenate(
                 [jnp.where(high == t, got, 0.0).astype(jnp.bfloat16) for t in range(tiles)], axis=0
             )
-            low = jnp.where(low_iota == target % LANES, 1.0, 0.0).astype(jnp.bfloat16)
+            low = jnp.where(low_iota == (target & (LANES - 1)), 1.0, 0.0).astype(jnp.bfloat16)
             link_part[...] += lax.dot_general(
                 spread, low, (((1,), (1,)), ((), ())), preferred_element_type=jnp.float32
             )
@@ -300,7 +331,8 @@
         total = total + stat_in[step]
     sums = jnp.sum(total, axis=1, keepdims=True)
     norms = jnp.sqrt(sums[PAD:]) / jnp.sqrt(sums[:PAD] + 1.0)
-    norm_out[...] = jnp.broadcast_to(norms, norm_out.shape)
+    norms = jnp.where(diag, jnp.broadcast_to(norms, (PAD, vector_part)), 0.0)
+    norm_out[...] = jnp.sum(norms, axis=0, keepdims=True)
 
     each(0, planes, lambda plane: mate_copy(plane).wait_send())
     each(0, planes, lambda plane: wire_copy(plane).wait_send())
@@ -322,33 +354,11 @@
     upper_cells,
 ):
     count = lax.axis_size("rows")
-    vec = lax.axis_index("vecs")
     vector_part = eigen_values.shape[0]
     rank_part, rows_local = basis.shape
     cells = WID * WID
     planes = rows_local // cells
     slots = lower_cells.shape[1]
-    mate = vec + 1 - 2 * (vec % 2)
-    across = (vec + 2) % 4
-
-    def factor(rank_owner, vector_owner):
-        piece = lax.dynamic_slice(
-            coefficients,
-            (rank_owner * rank_part, vector_owner * vector_part),
-            (rank_part, vector_part),
-        )
-        return jnp.pad(piece.T, ((0, PAD - vector_part), (0, 0)))
-
-    factors = jnp.stack(
-        [
-            jnp.concatenate([factor(owner, vec), factor(owner, across)], axis=0)
-            for owner in (vec, mate)
-        ]
-    )
-    eigen = jnp.pad(eigen_values, (0, PAD - vector_part))[:, None]
-    used = jnp.arange(slots, dtype=jnp.int32) < link_count[0]
-    links = jnp.where(used[None, :], jnp.concatenate([lower_cells, upper_cells]), -1)
-    links = jnp.pad(links, ((0, 6), (0, 0)), constant_values=-1)
     vmem = pl.BlockSpec(memory_space=pltpu.VMEM)
     wire = cells // 2 + cells // 8
     dma = pltpu.SemaphoreType.DMA
@@ -357,9 +367,9 @@
         out_shape=(
             jax.ShapeDtypeStruct((vector_part, rows_local), jnp.bfloat16),
             jax.ShapeDtypeStruct((vector_part, rows_local), jnp.bfloat16),
-            jax.ShapeDtypeStruct((PAD, LANES), jnp.float32),
+            jax.ShapeDtypeStruct((1, vector_part), jnp.float32),
         ),
-        in_specs=[pl.BlockSpec(memory_space=pl.ANY)] + [vmem] * 6,
+        in_specs=[pl.BlockSpec(memory_space=pl.ANY)] + [vmem] * 5 + [pl.BlockSpec(memory_space=pltpu.SMEM), vmem, vmem],
         out_specs=(vmem, vmem, vmem),
         scratch_shapes=[
             pltpu.VMEM((rank_part, rows_local), jnp.bfloat16),
@@ -374,6 +384,8 @@
             pltpu.VMEM((cells // LANES * PAD, LANES), jnp.float32),
             pltpu.VMEM((2 * PAD, LANES), jnp.float32),
             pltpu.VMEM((count, 2 * PAD, LANES), jnp.float32),
+            pltpu.VMEM((8, slots), jnp.int32),
+            pltpu.VMEM((2, 2 * PAD, rank_part), jnp.bfloat16),
             dma((planes,)),
             dma((planes,)),
             dma((planes,)),
@@ -389,14 +401,16 @@
         ),
     )(
         basis,
-        factors,
-        eigen,
+        coefficients.T,
+        eigen_values[None, :],
         stiffness[None, :],
         damping[None, :],
         mass[None, :],
-        links,
+        link_count,
+        lower_cells,
+        upper_cells,
     )
-    return eigvecs, residuals, norms[:vector_part, 0]
+    return eigvecs, residuals, norms[0]
 
 
 def solution(mesh):

time: 59.1 us -> 53.7 us (0.909)
  local copies, waits for them, and re-layouts: 8.76 us -> 5.03 us
  other arithmetic: 1.41 us -> 0 us
    broadcast_in_dim x2 -> x0, local copies, waits for them, and re-layouts: 1.34 us -> none  [on_device(): eigen = jnp.pad(eigen_values, (0, PAD - vector_part))[:, None]]
    slice x1 -> x0, local copies, waits for them, and re-layouts: 1.32 us -> none  [on_device(): return (eigvecs, residuals, norms[:vector_part, 0])]
    transpose x1 -> x0, local copies, waits for them, and re-layouts: 0.92 us -> none  [factor(): return jnp.pad(piece.T, ((0, PAD - vector_part), (0, 0)))]
    select_n x1 -> x0, other arithmetic: 0.78 us -> none  [on_device(): jnp.where(used[None, :], jnp.concatenate([lower_cells, upper_cells]), -1)]
    pad x1 -> x0, local copies, waits for them, and re-layouts: 0.67 us -> none  [on_device(): links = jnp.pad(links, ((0, 6), (0, 0)), constant_values=-1)]
    another operation x2 -> x0, other arithmetic: 0.62 us -> none  [on_device(): jnp.stack([jnp.concatenate([factor(owner, vec), factor(owner, across)], a...]
    unnamed x4 -> x7, local copies, waits for them, and re-layouts: 4.52 us -> 5.03 us
where the time goes in v2:
time: 53.7 us; the launch traced here: 53.5 us
  Pallas kernels  47.2 us (88%)
  local copies, waits for them, and re-layouts  5.03 us (9%)
  between operations  1.3 us (2%)
    pallas_call x1, Pallas kernels, on_device(): pl.pallas_call(functools.partial(kernel, count, planes, cells, vector_par...  47.2 us
    unnamed x7, local copies, waits for them, and re-layouts  5.03 us

profile of v2, /device:TPU:0, one launch (start us, length us, event | category | flops | bytes accessed | tf_op | source)
XLA Modules:
  0.0 53.5 jit_solution(4276065007543072990)
XLA Ops:
  1.3 47.2 %shard_map.112 = (bf16[10,65536]{1,0:T(8,128)(2,1)}, bf16[10,65536]{1,0:T(8,128)(2,1)}, f32[1,10]{1,0:T(1,128)}) custom-call(bf16[25,65536]{1,0:T(8,128)(2,1)} %basis.1, bf16[40,100]{1,0:T(8,128)(2,1)} %bitcast.9, f32[1,10]{1,0:T(1,128)} %bitcast.10, f32[1,65536]{1,0:T(1,128)} %bitcast.6, f32[1,65536]{1,0:T(1,128)} %bitcast.7, f32[1,65536]{1,0:T(1,128)} %bitcast.8, ...), custom_call_target="tpu_custom_call" | custom-call | tf_op jit(solution)/shard_map/pallas_call | solution.py:365
  48.5 0.0 copy-start
  48.5 3.2 %copy.16 = bf16[10,65536]{1,0:T(8,128)(2,1)} copy(bf16[10,65536]{1,0:T(8,128)(2,1)} %get-tuple-element.12) | data formatting | bytes 2621440
  51.7 0.0 copy-done
  51.7 0.0 copy-start.1
  51.7 1.3 %copy.17 = bf16[10,65536]{1,0:T(8,128)(2,1)} copy(bf16[10,65536]{1,0:T(8,128)(2,1)S(1)} %copy-done) | data formatting | bytes 2621440
  53.0 0.0 copy-done.1
  53.0 0.5 copy.18
Async XLA Ops:
  48.5 3.2 %copy-start = (bf16[10,65536]{1,0:T(8,128)(2,1)S(1)}, bf16[10,65536]{1,0:T(8,128)(2,1)}, u32[]{:S(2)}) copy-start(bf16[10,65536]{1,0:T(8,128)(2,1)} %get-tuple-element.13) | copy-start | bytes 3932164
  51.7 1.3 %copy-start.1 = (f32[1,10]{1,0:T(1,128)S(1)}, f32[1,10]{1,0:T(1,128)}, u32[]{:S(2)}) copy-start(f32[1,10]{1,0:T(1,128)} %get-tuple-element.8) | copy-start | bytes 124

commit v3 on v2

--- a/solution.py
+++ b/solution.py
@@ -33,9 +33,9 @@
     basis,
     coefficients,
     eigen,
-    stiffness,
-    damping,
-    mass,
+    stiffness_in,
+    damping_in,
+    mass_in,
     used,
     lower,
     upper,
@@ -56,6 +56,11 @@
     stat_in,
     links,
     factors,
+    stiffness,
+    damping,
+    mass,
+    stat_line,
+    input_sem,
     local_sem,
     mate_send,
     mate_recv,
@@ -116,7 +121,7 @@
 
     def stat_copy(step):
         return remote(
-            stat_out,
+            stat_line,
             stat_in.at[step],
             stat_send.at[step],
             stat_recv.at[step],
@@ -131,6 +136,14 @@
         lax.fori_loop(first, last, run, 0)
 
     each(0, planes, lambda step: local_copy(plane_at(step)).start())
+    diagonals = [
+        pltpu.make_async_copy(source, target, input_sem.at[place])
+        for place, (source, target) in enumerate(
+            ((stiffness_in, stiffness), (damping_in, damping), (mass_in, mass))
+        )
+    ]
+    for copy in diagonals:
+        copy.start()
 
     barrier = pltpu.get_barrier_semaphore()
 
@@ -200,6 +213,8 @@
         wire_copy(plane).start()
 
     each(0, planes, produce)
+    for copy in diagonals:
+        copy.wait()
 
     def fold(block):
         total = block[:, :LANES]
@@ -311,7 +326,7 @@
         finish(plane)
         stencil(plane - 1, None)
 
-    middle = max(2, planes // 2 - 1)
+    middle = min(4, planes - 1)
     each(2, middle, advance)
     face_copy(0).wait_recv()
     links_copy().wait_recv()
@@ -323,22 +338,23 @@
     stencil(planes - 2, None)
     stencil(planes - 1, 1)
 
+    sums = jnp.sum(stat_out[...], axis=1, keepdims=True)
+    spot = lax.broadcasted_iota(jnp.int32, (2 * PAD, LANES), 0) == lax.broadcasted_iota(
+        jnp.int32, (2 * PAD, LANES), 1
+    )
+    line = jnp.sum(jnp.where(spot, sums, 0.0), axis=0, keepdims=True)
+    stat_line[...] = line
     each(1, count, lambda step: stat_copy(step).start())
-    stat_in[0] = stat_out[...]
-    each(1, count, lambda step: stat_copy(step).wait_recv())
-    total = stat_in[0]
-    for step in range(1, count):
-        total = total + stat_in[step]
-    sums = jnp.sum(total, axis=1, keepdims=True)
-    norms = jnp.sqrt(sums[PAD:]) / jnp.sqrt(sums[:PAD] + 1.0)
-    norms = jnp.where(diag, jnp.broadcast_to(norms, (PAD, vector_part)), 0.0)
-    norm_out[...] = jnp.sum(norms, axis=0, keepdims=True)
-
     each(0, planes, lambda plane: mate_copy(plane).wait_send())
     each(0, planes, lambda plane: wire_copy(plane).wait_send())
     links_copy().wait_send()
     face_copy(0).wait_send()
     face_copy(1).wait_send()
+    each(1, count, lambda step: stat_copy(step).wait_recv())
+    for step in range(1, count):
+        line = line + stat_in[step]
+    norms = jnp.sqrt(line[:, PAD : PAD + vector_part]) / jnp.sqrt(line[:, :vector_part] + 1.0)
+    norm_out[...] = norms
     each(1, count, lambda step: stat_copy(step).wait_send())
 
 
@@ -360,16 +376,17 @@
     planes = rows_local // cells
     slots = lower_cells.shape[1]
     vmem = pl.BlockSpec(memory_space=pltpu.VMEM)
+    anywhere = pl.BlockSpec(memory_space=pltpu.HBM)
     wire = cells // 2 + cells // 8
     dma = pltpu.SemaphoreType.DMA
     eigvecs, residuals, norms = pl.pallas_call(
         functools.partial(kernel, count, planes, cells, vector_part),
         out_shape=(
-            jax.ShapeDtypeStruct((vector_part, rows_local), jnp.bfloat16),
-            jax.ShapeDtypeStruct((vector_part, rows_local), jnp.bfloat16),
+            pltpu.VMEM((vector_part, rows_local), jnp.bfloat16),
+            pltpu.VMEM((vector_part, rows_local), jnp.bfloat16),
             jax.ShapeDtypeStruct((1, vector_part), jnp.float32),
         ),
-        in_specs=[pl.BlockSpec(memory_space=pl.ANY)] + [vmem] * 5 + [pl.BlockSpec(memory_space=pltpu.SMEM), vmem, vmem],
+        in_specs=[anywhere, vmem, vmem, anywhere, anywhere, anywhere] + [pl.BlockSpec(memory_space=pltpu.SMEM), vmem, vmem],
         out_specs=(vmem, vmem, vmem),
         scratch_shapes=[
             pltpu.VMEM((rank_part, rows_local), jnp.bfloat16),
@@ -383,9 +400,14 @@
             pltpu.VMEM((2, PAD, cells), jnp.float32),
             pltpu.VMEM((cells // LANES * PAD, LANES), jnp.float32),
             pltpu.VMEM((2 * PAD, LANES), jnp.float32),
-            pltpu.VMEM((count, 2 * PAD, LANES), jnp.float32),
+            pltpu.VMEM((count, 1, LANES), jnp.float32),
             pltpu.VMEM((8, slots), jnp.int32),
             pltpu.VMEM((2, 2 * PAD, rank_part), jnp.bfloat16),
+            pltpu.VMEM((1, rows_local), jnp.float32),
+            pltpu.VMEM((1, rows_local), jnp.float32),
+            pltpu.VMEM((1, rows_local), jnp.float32),
+            pltpu.VMEM((1, LANES), jnp.float32),
+            dma((3,)),
             dma((planes,)),
             dma((planes,)),
             dma((planes,)),

time: 53.7 us -> 48.8 us (0.909)
  Pallas kernels: 47.2 us -> 44.1 us
  local copies, waits for them, and re-layouts: 5.03 us -> 3.16 us
    pallas_call x1, Pallas kernels: 47.2 us -> 44.1 us  [on_device(): pl.pallas_call(functools.partial(kernel, count, planes, cells, vector_par...]
    unnamed x7 -> x5, local copies, waits for them, and re-layouts: 5.03 us -> 3.16 us
where the time goes in v3:
time: 48.8 us; the launch traced here: 48.6 us
  Pallas kernels  44.1 us (90%)
  local copies, waits for them, and re-layouts  3.16 us (6%)
  between operations  1.29 us (3%)
    pallas_call x1, Pallas kernels, on_device(): pl.pallas_call(functools.partial(kernel, count, planes, cells, vector_par...  44.1 us
    unnamed x5, local copies, waits for them, and re-layouts  3.16 us

profile of v3, /device:TPU:0, one launch (start us, length us, event | category | flops | bytes accessed | tf_op | source)
XLA Modules:
  0.0 48.6 jit_solution(3150516193316558825)
XLA Ops:
  1.3 44.1 %shard_map.112 = (bf16[10,65536]{1,0:T(8,128)(2,1)S(1)}, bf16[10,65536]{1,0:T(8,128)(2,1)S(1)}, f32[1,10]{1,0:T(1,128)}) custom-call(bf16[25,65536]{1,0:T(8,128)(2,1)} %basis.1, bf16[40,100]{1,0:T(8,128)(2,1)} %bitcast.9, f32[1,10]{1,0:T(1,128)} %bitcast.10, f32[1,65536]{1,0:T(1,128)} %bitcast.6, f32[1,65536]{1,0:T(1,128)} %bitcast.7, f32[1,65536]{1,0:T(1,128)} %bitcast.8, ...), custom_call_target="tpu_custom_call" | custom-call | tf_op jit(solution)/shard_map/pallas_call | solution.py:382
  45.4 1.3 %copy.15 = bf16[10,65536]{1,0:T(8,128)(2,1)} copy(bf16[10,65536]{1,0:T(8,128)(2,1)S(1)} %get-tuple-element.9) | data formatting | bytes 2621440
  46.7 0.0 copy-start
  46.7 1.3 %copy.16 = bf16[10,65536]{1,0:T(8,128)(2,1)} copy(bf16[10,65536]{1,0:T(8,128)(2,1)S(1)} %get-tuple-element.10) | data formatting | bytes 2621440
  48.0 0.0 copy-done
  48.1 0.5 %copy.18 = f32[10]{0:T(128)} copy(f32[10]{0:T(128)S(1)} %bitcast.11) | data formatting | bytes 80
Async XLA Ops:
  46.7 1.3 %copy-start = (f32[1,10]{1,0:T(1,128)S(1)}, f32[1,10]{1,0:T(1,128)}, u32[]{:S(2)}) copy-start(f32[1,10]{1,0:T(1,128)} %get-tuple-element.8) | copy-start | bytes 124

commit v4 on v3

--- a/solution.py
+++ b/solution.py
@@ -31,14 +31,14 @@
     cells,
     vector_part,
     basis,
-    coefficients,
-    eigen,
+    coefficients_in,
+    eigen_in,
     stiffness_in,
     damping_in,
     mass_in,
-    used,
-    lower,
-    upper,
+    used_in,
+    lower_in,
+    upper_in,
     eig_out,
     res_out,
     norm_out,
@@ -60,6 +60,11 @@
     damping,
     mass,
     stat_line,
+    coefficients,
+    eigen,
+    used,
+    lower,
+    upper,
     input_sem,
     local_sem,
     mate_send,
@@ -95,7 +100,7 @@
 
     def mate_copy(plane):
         return remote(
-            basis.at[:, lanes_of(plane)],
+            own_basis.at[:, lanes_of(plane)],
             mate_basis.at[:, lanes_of(plane)],
             mate_send.at[plane],
             mate_recv.at[plane],
@@ -135,24 +140,40 @@
 
         lax.fori_loop(first, last, run, 0)
 
-    each(0, planes, lambda step: local_copy(plane_at(step)).start())
-    diagonals = [
+    barrier = pltpu.get_barrier_semaphore()
+
+    def greet(where):
+        pl.semaphore_signal(barrier, inc=1, device_id=where, device_id_type=pl.DeviceIdType.MESH)
+
+    each(1, count, lambda step: greet({"rows": (row + step) % count}))
+    greet(mate)
+    greet(across)
+
+    inputs = [
         pltpu.make_async_copy(source, target, input_sem.at[place])
         for place, (source, target) in enumerate(
-            ((stiffness_in, stiffness), (damping_in, damping), (mass_in, mass))
+            (
+                (coefficients_in, coefficients),
+                (eigen_in, eigen),
+                (used_in, used),
+                (lower_in, lower),
+                (upper_in, upper),
+                (stiffness_in, stiffness),
+                (damping_in, damping),
+                (mass_in, mass),
+            )
         )
     ]
-    for copy in diagonals:
+    for copy in inputs[:5]:
         copy.start()
-
-    barrier = pltpu.get_barrier_semaphore()
-
-    def greet(where):
-        pl.semaphore_signal(barrier, inc=1, device_id=where, device_id_type=pl.DeviceIdType.MESH)
-
-    greet(mate)
-    greet(across)
-    each(1, count, lambda step: greet({"rows": (row + step) % count}))
+    each(0, planes, lambda step: local_copy(plane_at(step)).start())
+    for copy in inputs[5:]:
+        copy.start()
+
+    values[...] = jnp.zeros_like(values)
+    stat_out[...] = jnp.zeros_like(stat_out)
+    for copy in inputs[:5]:
+        copy.wait()
 
     slot = lax.broadcasted_iota(jnp.int32, (1, slots), 1)
     is_used = slot < used[0]
@@ -176,11 +197,13 @@
         part = jnp.dot(chosen, pick, preferred_element_type=jnp.float32)
         factors[side] = part.astype(jnp.bfloat16)
 
-    values[...] = jnp.zeros_like(values)
-    stat_out[...] = jnp.zeros_like(stat_out)
     pl.semaphore_wait(barrier, count + 1)
 
-    each(0, planes, lambda step: mate_copy(plane_at(step)).start())
+    def pass_on(step):
+        local_copy(plane_at(step)).wait()
+        mate_copy(plane_at(step)).start()
+
+    each(0, planes, pass_on)
     links_copy().start()
 
     row_iota = lax.broadcasted_iota(jnp.int32, (FULL, eighth), 0)
@@ -188,7 +211,6 @@
 
     def produce(step):
         plane = plane_at(step)
-        local_copy(plane).wait()
         mate_copy(plane).wait_recv()
         both = jnp.dot(
             factors[0], own_basis[:, lanes_of(plane)], preferred_element_type=jnp.float32
@@ -213,7 +235,7 @@
         wire_copy(plane).start()
 
     each(0, planes, produce)
-    for copy in diagonals:
+    for copy in inputs[5:]:
         copy.wait()
 
     def fold(block):
@@ -356,6 +378,19 @@
     norms = jnp.sqrt(line[:, PAD : PAD + vector_part]) / jnp.sqrt(line[:, :vector_part] + 1.0)
     norm_out[...] = norms
     each(1, count, lambda step: stat_copy(step).wait_send())
+
+
+def write_back(eig_held, res_held, norm_held, eig_out, res_out, norm_out, sem):
+    copies = [
+        pltpu.make_async_copy(source, target, sem.at[place])
+        for place, (source, target) in enumerate(
+            ((eig_held, eig_out), (res_held, res_out), (norm_held, norm_out))
+        )
+    ]
+    for copy in copies:
+        copy.start()
+    for copy in copies:
+        copy.wait()
 
 
 def on_device(
@@ -384,9 +419,9 @@
         out_shape=(
             pltpu.VMEM((vector_part, rows_local), jnp.bfloat16),
             pltpu.VMEM((vector_part, rows_local), jnp.bfloat16),
-            jax.ShapeDtypeStruct((1, vector_part), jnp.float32),
+            pltpu.VMEM((1, vector_part), jnp.float32),
         ),
-        in_specs=[anywhere, vmem, vmem, anywhere, anywhere, anywhere] + [pl.BlockSpec(memory_space=pltpu.SMEM), vmem, vmem],
+        in_specs=[anywhere] * 9,
         out_specs=(vmem, vmem, vmem),
         scratch_shapes=[
             pltpu.VMEM((rank_part, rows_local), jnp.bfloat16),
@@ -407,7 +442,12 @@
             pltpu.VMEM((1, rows_local), jnp.float32),
             pltpu.VMEM((1, rows_local), jnp.float32),
             pltpu.VMEM((1, LANES), jnp.float32),
-            dma((3,)),
+            pltpu.VMEM(coefficients.shape[::-1], jnp.bfloat16),
+            pltpu.VMEM((1, vector_part), jnp.float32),
+            pltpu.SMEM((1,), jnp.int32),
+            pltpu.VMEM((1, slots), jnp.int32),
+            pltpu.VMEM((1, slots), jnp.int32),
+            dma((8,)),
             dma((planes,)),
             dma((planes,)),
             dma((planes,)),
@@ -432,6 +472,16 @@
         lower_cells,
         upper_cells,
     )
+    eigvecs, residuals, norms = pl.pallas_call(
+        write_back,
+        out_shape=tuple(
+            jax.ShapeDtypeStruct(held.shape, held.dtype) for held in (eigvecs, residuals, norms)
+        ),
+        in_specs=[vmem] * 3,
+        out_specs=[pl.BlockSpec(memory_space=pl.ANY)] * 3,
+        scratch_shapes=[dma((3,))],
+        compiler_params=pltpu.CompilerParams(vmem_limit_bytes=1 << 20),
+    )(eigvecs, residuals, norms)
     return eigvecs, residuals, norms[0]
 
 

time: 48.8 us -> 46.8 us (0.959)
  local copies, waits for them, and re-layouts: 3.16 us -> 0 us
  Pallas kernels: 44.1 us -> 45.3 us
    unnamed x5 -> x0, local copies, waits for them, and re-layouts: 3.16 us -> none
    pallas_call x0 -> x1, Pallas kernels: none -> 2.04 us  [on_device(): pl.pallas_call(write_back, out_shape=tuple((jax.ShapeDtypeStruct(held.sha...]
    pallas_call x1, Pallas kernels: 44.1 us -> 43.2 us  [on_device(): pl.pallas_call(functools.partial(kernel, count, planes, cells, vector_par...]
where the time goes in v4:
time: 46.8 us; the launch traced here: 46.5 us
  Pallas kernels  45.3 us (97%)
  between operations  1.29 us (3%)
    pallas_call x1, Pallas kernels, on_device(): pl.pallas_call(functools.partial(kernel, count, planes, cells, vector_par...  43.2 us
    pallas_call x1, Pallas kernels, on_device(): pl.pallas_call(write_back, out_shape=tuple((jax.ShapeDtypeStruct(held.sha...  2.04 us

profile of v4, /device:TPU:0, one launch (start us, length us, event | category | flops | bytes accessed | tf_op | source)
XLA Modules:
  0.0 46.5 jit_solution(1872774099023987617)
XLA Ops:
  1.3 43.2 %shard_map.112 = (bf16[10,65536]{1,0:T(8,128)(2,1)S(1)}, bf16[10,65536]{1,0:T(8,128)(2,1)S(1)}, f32[1,10]{1,0:T(1,128)S(1)}) custom-call(bf16[25,65536]{1,0:T(8,128)(2,1)} %basis.1, bf16[40,100]{1,0:T(8,128)(2,1)} %bitcast.9, f32[1,10]{1,0:T(1,128)} %bitcast.10, f32[1,65536]{1,0:T(1,128)} %bitcast.6, f32[1,65536]{1,0:T(1,128)} %bitcast.7, ...), custom_call_target="tpu_custom_call" | custom-call | tf_op jit(solution)/shard_map/pallas_call | solution.py:417
  44.5 2.0 %shard_map.113 = (bf16[10,65536]{1,0:T(8,128)(2,1)}, bf16[10,65536]{1,0:T(8,128)(2,1)}, f32[1,10]{1,0:T(1,128)}) custom-call(bf16[10,65536]{1,0:T(8,128)(2,1)S(1)} %get-tuple-element.9.eig_held, bf16[10,65536]{1,0:T(8,128)(2,1)S(1)} %get-tuple-element.10.res_held, f32[1,10]{1,0:T(1,128)S(1)} %get-tuple-element.11.norm_held), custom_call_target="tpu_custom_call" | custom-call | tf_op jit(solution)/shard_map/pallas_call | solution.py:475
